TPU v7x, 1024 devices: a whole 8x8x8 slice. The times are simulated.
1024 devices in a mesh: tile: 4 (over y_lo), seq: 8 (over z), group: 32 (over x, y_hi, core).
Axes of the slice: x: 8, y: 8 (y_hi: 2, y_lo: 4; y = y_hi * 4 + y_lo), z: 8, core: 2. Of those that a mesh axis runs over, the one named last changes fastest.
Arguments:
- features: bfloat16 [8, 32, 2, 16, 64, 512], P('seq', 'group', None, 'tile'), may hold values from -6 to 6
- conv_weight: bfloat16 [3, 3, 3, 512, 16], replicated, may hold values from -0.0546875 to 0.0546875
- conv_bias: float32 [16], replicated, may hold values from -3 to 3
- embed_qkv: bfloat16 [64, 4608], replicated, may hold values from -0.75 to 0.75
- query_gain: float32 [128], replicated, may hold values from 0.5 to 2
- key_gain: float32 [128], replicated, may hold values from 0.5 to 2
- bucket: int32 [8, 32], replicated, may hold values from 0 to 31, as said below
- frames: int32 [8, 32], replicated, may hold values from 1 to 2
Outputs:
- attended: bfloat16 [8, 32, 2, 512, 1536], P('seq', 'group', None, 'tile')
Inputs may be any that keep to these rules, and one draw needn't show every extreme that they name: In each row every bucket receives at most 2 clips; exactly 8 buckets receive 2, and as many receive none.
All inputs are finite; a program needn't handle non-finite values.
Results may differ from a plain program's by a relative error of at most 0.0046.
Values may be sent and summed in bfloat16 or wider, within the bound.
A program may use at most 128 MiB of HBM per device.

v0:
```python
import math

import jax
import jax.numpy as jnp
from jax import lax
from jax.sharding import PartitionSpec as P

HEADS = 12
HEAD = 128
D = 1536
CAP = 2


def with_halo(block, sides, width):
    for axis, dim in sides:
        count = lax.axis_size(axis)
        forward = [(i, i + 1) for i in range(count - 1)]
        backward = [(target, source) for source, target in forward]
        low = lax.ppermute(
            lax.slice_in_dim(block, block.shape[dim] - width, None, axis=dim), axis, forward
        )
        high = lax.ppermute(lax.slice_in_dim(block, 0, width, axis=dim), axis, backward)
        block = jnp.concatenate([low, block, high], axis=dim)
    return block


def laid_out(parts, dim):
    shape = list(parts.shape[1:])
    shape[dim] *= parts.shape[0]
    return jnp.moveaxis(parts, 0, dim).reshape(shape)


def sent_to_all(x, axis):
    count = lax.axis_size(axis)
    return lax.all_to_all(jnp.broadcast_to(x[None], (count, *x.shape)), axis, 0, 0, tiled=True)


def gather_directly(x, axis, dim):
    return laid_out(sent_to_all(x, axis), dim)


def tap_products(padded, conv_weight):
    channels = padded.shape[-1]
    flat_weight = jnp.transpose(conv_weight, (3, 0, 1, 2, 4)).reshape(channels, -1)
    products = jnp.dot(
        padded.reshape(-1, channels), flat_weight, preferred_element_type=jnp.float32
    )
    return products.reshape(padded.shape[:-1] + (27, conv_weight.shape[-1]))


def tap_sum(products, frame_count, row_count, col_count):
    running = jnp.zeros((frame_count, row_count, col_count, products.shape[-1]), jnp.float32)
    for depth_tap in range(3):
        for row_tap in range(3):
            for col_tap in range(3):
                tap_index = depth_tap * 9 + row_tap * 3 + col_tap
                running = (
                    running
                    + products[
                        depth_tap : depth_tap + frame_count,
                        row_tap : row_tap + row_count,
                        col_tap : col_tap + col_count,
                        tap_index,
                    ]
                )
    return running


def edge_sum(products, row_at, row_tap, frame_count, col_count):
    running = jnp.zeros((frame_count, col_count, products.shape[-1]), jnp.float32)
    for depth_tap in range(3):
        for col_tap in range(3):
            tap_index = depth_tap * 9 + row_tap * 3 + col_tap
            running = (
                running
                + products[
                    depth_tap : depth_tap + frame_count,
                    row_at,
                    col_tap : col_tap + col_count,
                    tap_index,
                ]
            )
    return running


def head_norm(values, gain_vec, head_size):
    shaped = values.reshape(values.shape[:-1] + (-1, head_size))
    scaled = shaped * lax.rsqrt(jnp.mean(shaped * shaped, axis=-1, keepdims=True) + 1e-06)
    return scaled * gain_vec


def attend(queries, key_rows, value_rows, key_valid):
    scores = jnp.einsum("qhe,khe->hqk", queries, key_rows, preferred_element_type=jnp.float32)
    scores = jnp.where(key_valid[None, None, :], scores, -1e30)
    row_max = jnp.max(scores, axis=-1, keepdims=True)
    weights = jnp.exp(scores - row_max)
    totals = jnp.sum(weights, axis=-1)
    mixed_out = jnp.einsum(
        "hqk,khe->qhe", weights.astype(jnp.bfloat16), value_rows, preferred_element_type=jnp.float32
    )
    return mixed_out / jnp.transpose(totals)[:, :, None]


def shards(features, conv_weight, conv_bias, embed_qkv, query_gain, key_gain, bucket, frames):
    local_block = features[0, 0]
    frame_count, row_count, col_count, channels = local_block.shape
    tile_here = lax.axis_index("tile")
    is_first = tile_here == 0
    is_last = tile_here == lax.axis_size("tile") - 1
    padded = jnp.pad(local_block, ((2, 0), (0, 0), (1, 1), (0, 0)), mode="edge")
    products = tap_products(padded, conv_weight)
    interior = tap_sum(
        jnp.pad(products, ((0, 0), (1, 1), (0, 0), (0, 0), (0, 0))),
        frame_count,
        row_count,
        col_count,
    )
    to_prev = edge_sum(products, 0, 2, frame_count, col_count)
    to_next = edge_sum(products, row_count - 1, 0, frame_count, col_count)
    borders = with_halo(jnp.stack([to_prev, to_next]), (("tile", 0),), 1)
    top_term = jnp.where(is_first, edge_sum(products, 0, 0, frame_count, col_count), borders[0])
    bottom_term = jnp.where(
        is_last, edge_sum(products, row_count - 1, 2, frame_count, col_count), borders[3]
    )
    summed = interior.at[:, 0].add(top_term).at[:, row_count - 1].add(bottom_term)
    latent = (summed + conv_bias).astype(jnp.bfloat16)
    latent_channels = latent.shape[-1]
    tokens = latent.reshape(frame_count, row_count // 2, 2, col_count // 2, 2, latent_channels)
    tokens = jnp.transpose(tokens, (0, 1, 3, 2, 4, 5)).reshape(-1, 4 * latent_channels)
    groups = lax.axis_size("group")
    group_here = lax.axis_index("group")
    bucket_row = lax.dynamic_index_in_dim(bucket, lax.axis_index("seq"), 0, keepdims=False)
    frame_row = lax.dynamic_index_in_dim(frames, lax.axis_index("seq"), 0, keepdims=False)
    order_ids = jnp.arange(groups, dtype=jnp.int32)
    same_bucket = bucket_row[:, None] == bucket_row[None, :]
    earlier = order_ids[None, :] < order_ids[:, None]
    slot_of = jnp.sum(jnp.where(same_bucket & earlier, 1, 0), axis=1).astype(jnp.int32)
    slot_ids = jnp.arange(CAP, dtype=jnp.int32)
    picked = (bucket_row[None, :] == group_here) & (slot_of[None, :] == slot_ids[:, None])
    selector = picked.astype(jnp.bfloat16)
    filled = jnp.sum(jnp.where(picked, 1, 0), axis=1)
    slot_frames = jnp.sum(jnp.where(picked, frame_row[None, :], 0), axis=1)
    destination = lax.dynamic_index_in_dim(bucket_row, group_here, 0, keepdims=False)
    outgoing = jnp.where(
        (order_ids == destination)[:, None, None], tokens[None], jnp.zeros((), jnp.bfloat16)
    )
    incoming = lax.all_to_all(outgoing, "group", split_axis=0, concat_axis=0, tiled=True)
    gathered = jnp.einsum("cg,gtf->ctf", selector, incoming, preferred_element_type=jnp.float32)
    slots = gathered.astype(jnp.bfloat16)
    query_weight = embed_qkv[:, :D]
    pair_weight = embed_qkv[:, D:]
    flat_rows = gather_directly(slots, "tile", 1)
    projected = jnp.einsum(
        "ctf,fe->cte", flat_rows, pair_weight, preferred_element_type=jnp.float32
    )
    normed = (
        head_norm(projected[..., :D], key_gain, HEAD)
        .reshape(projected.shape[:-1] + (D,))
        .astype(jnp.bfloat16)
    )
    key_values = jnp.concatenate([normed, projected[..., D:].astype(jnp.bfloat16)], axis=-1)
    query_full = jnp.einsum("ctf,fe->cte", slots, query_weight, preferred_element_type=jnp.float32)
    queries = (head_norm(query_full, query_gain, HEAD) / math.sqrt(HEAD)).astype(jnp.bfloat16)
    token_count = slots.shape[1]
    per_frame = row_count // 2 * (col_count // 2)
    clip_tokens = key_values.shape[1]
    key_frame = jnp.arange(clip_tokens, dtype=jnp.int32) % token_count // per_frame
    query_frame = jnp.arange(token_count, dtype=jnp.int32) // per_frame
    outputs = []
    for slot_at in range(CAP):
        key_rows = key_values[slot_at, :, :D].reshape(clip_tokens, HEADS, HEAD)
        value_rows = key_values[slot_at, :, D:].reshape(clip_tokens, HEADS, HEAD)
        mixed_out = attend(queries[slot_at], key_rows, value_rows, key_frame < slot_frames[slot_at])
        query_keep = (query_frame < slot_frames[slot_at]) & (filled[slot_at] > 0)
        outputs.append(
            jnp.where(query_keep[:, None], mixed_out.reshape(token_count, D), 0.0).astype(
                jnp.bfloat16
            )
        )
    return jnp.stack(outputs)[None, None]


def solution(mesh):
    in_specs = (P("seq", "group", None, "tile", None, None), P(), P(), P(), P(), P(), P(), P())
    out_specs = P("seq", "group", None, "tile", None)
    return jax.shard_map(shards, mesh=mesh, in_specs=in_specs, out_specs=out_specs, check_vma=False)
```

profile of v0, /device:TPU:2, one launch (start us, length us, event | category | flops | bytes accessed | tf_op | source)
XLA Modules:
  0.0 127.7 jit_solution(868406622180521884)
XLA Ops:
  0.0 1.0 slice_bitcast_fusion.4
  1.1 2.9 %fusion.28 = f32[4,4,66,27,16]{2,3,4,1,0:T(8,128)S(1)} fusion(bf16[2,4,64,512]{3,2,1,0:T(8,128)(2,1)} %bitcast.235, bf16[2,4,64,512]{3,2,1,0:T(8,128)(2,1)S(1)} %reshape.582, bf16[27,16,512,1,1]{2,1,0,4,3:T(8,128)(2,1)S(1)} %bitcast.223), kind=kOutput, calls=%fused_computation.50 | convolution fusion | flops 476872704 | bytes 3315712 | tf_op jit(solution)/shard_map/dot_general | solution.py:45
  4.5 3.6 %collective-permute-start = (f32[1,2,64,16]{2,3,1,0:T(8,128)S(1)}, f32[1,2,64,16]{2,3,1,0:T(8,128)S(1)}, u32[]{:S(2)}, u32[]{:S(2)}) collective-permute-start(f32[1,2,64,16]{2,3,1,0:T(8,128)S(1)} %add_bitcast_fusion), channel_id=1, source_target_pairs={{0,256},{256,512},{512,768},{1,257},{257,513},{513,769},{2,258},{2... | collective-permute-start | bytes 24584 | tf_op jit(solution)/shard_map/ppermute | solution.py:19
  8.6 1.3 %collective-permute-start.1 = (f32[1,2,64,16]{2,3,1,0:T(8,128)S(1)}, f32[1,2,64,16]{2,3,1,0:T(8,128)S(1)}, u32[]{:S(2)}, u32[]{:S(2)}) collective-permute-start(f32[1,2,64,16]{2,3,1,0:T(8,128)S(1)} %bitcast.263), channel_id=1, source_target_pairs={{256,0},{512,256},{768,512},{257,1},{513,257},{769,513},{258,2},{5... | collective-permute-start | bytes 24584 | tf_op jit(solution)/shard_map/ppermute | solution.py:22
  9.9 3.8 %copy.166 = f32[4,4,66,27,16]{2,4,0,1,3:T(8,128)} copy(f32[4,4,66,27,16]{2,3,4,1,0:T(8,128)S(1)} %fusion.28) | data formatting | bytes 3649536 | tf_op jit(solution)/shard_map/dot_general | solution.py:45
  15.1 1.7 %fusion.87 = f32[2,4,64,16]{2,3,0,1:T(8,128)S(1)} fusion(f32[4,4,66,27,16]{2,4,0,1,3:T(8,128)} %copy.166), kind=kLoop, calls=%fused_computation.109 | loop fusion | flops 212992 | bytes 4161536 | tf_op jit(solution)/shard_map/add | solution.py:58
  16.9 1.3 %dynamic_slice.13 = s32[1,1]{1,0:T(1,128)} dynamic-slice(s32[8,32]{1,0:T(8,128)} %param.18, s32[]{:T(128)S(6)} %select_n.130, s32[]{:T(128)S(6)} %select_n.132), dynamic_slice_sizes={1,1} | dynamic-slice | bytes 12 | tf_op jit(solution)/shard_map/jit(dynamic_index_in_dim)/dynamic_slice | solution.py:143
  19.4 0.9 broadcast_select_fusion
  20.3 14.4 %all-to-all-start = ((bf16[32,128,64]{1,2,0:T(8,128)(2,1)}), bf16[32,128,64]{1,2,0:T(8,128)(2,1)S(1)}, u32[]{:S(2)}, u32[]{:S(2)}) async-start(bf16[32,128,64]{1,2,0:T(8,128)(2,1)} %broadcast_select_fusion), calls=%async_computation | async-start | bytes 1048576 | tf_op jit(solution)/shard_map/all_to_all | solution.py:147
  39.5 1.3 compare_and_fusion
  40.8 14.0 %all-to-all-done = bf16[32,128,64]{1,2,0:T(8,128)(2,1)S(1)} async-done(((bf16[32,128,64]{1,2,0:T(8,128)(2,1)}), bf16[32,128,64]{1,2,0:T(8,128)(2,1)S(1)}, u32[]{:S(2)}, u32[]{:S(2)}) %all-to-all-start) | async-done | bytes 524320 | tf_op jit(solution)/shard_map/all_to_all | solution.py:147
  55.6 1.6 %copy.211 = f32[2,128,12,128]{3,1,2,0:T(8,128)} copy(f32[2,128,12,128]{1,3,2,0:T(8,128)S(1)} %bitcast.226) | data formatting | bytes 3145728 | tf_op jit(solution)/shard_map/reshape | solution.py:87
  58.0 3.9 %all-to-all-start.1 = ((bf16[4,2,128,64]{2,3,1,0:T(8,128)(2,1)}), bf16[4,2,128,64]{2,3,1,0:T(8,128)(2,1)S(1)}, u32[]{:S(2)}, u32[]{:S(2)}) async-start(bf16[4,2,128,64]{2,3,1,0:T(8,128)(2,1)} %broadcast_in_dim.130), calls=%async_computation.1 | async-start | bytes 262144 | tf_op jit(solution)/shard_map/all_to_all | solution.py:35
  62.0 1.9 %multiply_convert_fusion.1 = bf16[2,128,12,128]{3,1,2,0:T(8,128)(2,1)S(1)} fusion(f32[2,128,12,128]{3,1,2,0:T(8,128)} %copy.211, f32[128]{0:T(128)S(1)} %copy-done.7, f32[2,128,12]{1,2,0:T(8,128)S(1)} %add_rsqrt_fusion.1), kind=kLoop, calls=%fused_computation.40 | loop fusion | flops 1572864 | bytes 2372096 | tf_op jit(solution)/shard_map/convert_element_type | solution.py:163
  63.9 4.0 %all-to-all-done.1 = bf16[4,2,128,64]{2,3,1,0:T(8,128)(2,1)S(1)} async-done(((bf16[4,2,128,64]{2,3,1,0:T(8,128)(2,1)}), bf16[4,2,128,64]{2,3,1,0:T(8,128)(2,1)S(1)}, u32[]{:S(2)}, u32[]{:S(2)}) %all-to-all-start.1) | async-done | bytes 131104 | tf_op jit(solution)/shard_map/all_to_all | solution.py:35
  67.9 6.4 %fusion.115 = (bf16[2,512,3072]{2,1,0:T(8,128)(2,1)S(1)}, f32[2,512,3072]{2,1,0:T(8,128)}) fusion(bf16[64,4608]{1,0:T(8,128)(2,1)S(1)} %copy-done.4, bf16[4,2,128,64]{2,3,1,0:T(8,128)(2,1)S(1)} %all-to-all-done.1), kind=kOutput, calls=%fused_computation.185 | convolution fusion | flops 405798912 | bytes 19398656 | tf_op jit(solution)/shard_map/ctf,fe->cte/dot_general | solution.py:153
  74.3 1.4 %fusion.109 = (bf16[1,512,1536]{2,1,0:T(8,128)(2,1)S(1)}, bf16[1,512,1536]{2,1,0:T(8,128)(2,1)}) fusion(bf16[2,512,3072]{2,1,0:T(8,128)(2,1)S(1)} %get-tuple-element.67), kind=kLoop, calls=%fused_computation.179 | loop fusion | bytes 6291456 | tf_op jit(solution)/shard_map/slice | solution.py:172
  75.7 2.6 %copy.217 = bf16[1,512,1536]{1,2,0:T(8,128)(2,1)} copy(bf16[1,512,1536]{2,1,0:T(8,128)(2,1)} %get-tuple-element.32) | data formatting | bytes 3145728 | tf_op jit(solution)/shard_map/slice | solution.py:172
  78.4 6.0 %slice_multiply_fusion = f32[2,512,1536]{2,1,0:T(8,128)} fusion(f32[2,512,3072]{2,1,0:T(8,128)} %get-tuple-element.68), kind=kLoop, calls=%fused_computation.19 | loop fusion | flops 1572864 | bytes 12582912 | tf_op jit(solution)/shard_map/mul | solution.py:88
  84.4 6.6 %copy.212 = f32[2,512,1536]{1,2,0:T(8,128)} copy(f32[2,512,1536]{2,1,0:T(8,128)} %slice_multiply_fusion) | data formatting | bytes 12582912 | tf_op jit(solution)/shard_map/mul | solution.py:88
  91.0 3.6 %reduce_sum.67 = f32[2,512,12]{1,2,0:T(8,128)S(1)} reduce(f32[2,512,12,128]{1,3,2,0:T(8,128)} %bitcast.224, f32[]{:T(128)} %constant.152.clone.1), dimensions={3}, to_apply=%region_4.5 | reduce | flops 1560576 | bytes 6340612 | tf_op jit(solution)/shard_map/reduce_sum | solution.py:88
  94.6 3.4 %mul.56 = f32[2,512,12,128]{1,3,2,0:T(8,128)} broadcast(f32[2,512,12]{1,2,0:T(8,128)S(1)} %add_rsqrt_fusion), dimensions={0,1,2} | broadcast | bytes 6340608 | tf_op jit(solution)/shard_map/mul | solution.py:88
  98.0 6.6 %copy.213 = f32[2,512,1536]{2,1,0:T(8,128)} copy(f32[2,512,1536]{1,2,0:T(8,128)} %bitcast.225) | data formatting | bytes 12582912 | tf_op jit(solution)/shard_map/mul | solution.py:88
  104.6 6.2 %multiply_convert_fusion = bf16[2,512,1536]{2,1,0:T(8,128)(2,1)S(1)} fusion(f32[2,512,1536]{2,1,0:T(8,128)} %copy.213, f32[2,512,3072]{2,1,0:T(8,128)} %get-tuple-element.68, f32[1536]{0:T(1024)S(1)} %broadcast_bitcast_fusion), kind=kLoop, calls=%fused_computation.18 | loop fusion | flops 4718592 | bytes 15734784 | tf_op jit(solution)/shard_map/convert_element_type | solution.py:159
  110.8 1.9 %fusion.112 = (bf16[1,512,1536]{2,1,0:T(8,128)(2,1)}, bf16[1,512,1536]{2,1,0:T(8,128)(2,1)}) fusion(bf16[2,512,1536]{2,1,0:T(8,128)(2,1)S(1)} %multiply_convert_fusion), kind=kLoop, calls=%fused_computation.182 | loop fusion | bytes 6291456 | tf_op jit(solution)/shard_map/slice | solution.py:171
  112.7 2.6 %copy.218 = bf16[1,512,1536]{1,2,0:T(8,128)(2,1)} copy(bf16[1,512,1536]{2,1,0:T(8,128)(2,1)} %get-tuple-element.62) | data formatting | bytes 3145728 | tf_op jit(solution)/shard_map/slice | solution.py:171
  115.3 2.0 %select_reduce_fusion = (f32[12,128]{1,0:T(8,128)S(1)}, f32[12,128,512]{2,1,0:T(8,128)S(1)}) fusion(pred[512]{0:T(512)(128)(4,1)S(1)} %broadcast_compare_fusion, bf16[512,12,128]{0,2,1:T(8,128)(2,1)} %bitcast.229, bf16[2,128,12,128]{3,1,2,0:T(8,128)(2,1)S(1)} %multiply_convert_fusion.1), kind=kOutput, calls=%fused_computation.22 | convolution fusion | flops 202897920 | bytes 5118464 | tf_op jit(solution)/shard_map/qhe,khe->hqk/dot_general | solution.py:93
  117.3 1.0 fusion.2
  119.8 1.6 %copy.208 = bf16[1,512,1536]{1,2,0:T(8,128)(2,1)} copy(bf16[1,512,1536]{2,1,0:T(8,128)(2,1)S(1)} %get-tuple-element.31) | data formatting | bytes 3145728 | tf_op jit(solution)/shard_map/slice | solution.py:172
  121.4 1.9 %copy.214 = bf16[1,512,1536]{1,2,0:T(8,128)(2,1)S(1)} copy(bf16[1,512,1536]{2,1,0:T(8,128)(2,1)} %get-tuple-element.61) | data formatting | bytes 3145728 | tf_op jit(solution)/shard_map/slice | solution.py:171
  124.0 1.0 fusion
  126.7 0.9 maximum_bitcast_fusion
  (53 shorter events, 12.6 us)
Async XLA Ops:
  0.0 1.1 copy-start
  4.5 14.3 %collective-permute-start = (f32[1,2,64,16]{2,3,1,0:T(8,128)S(1)}, f32[1,2,64,16]{2,3,1,0:T(8,128)S(1)}, u32[]{:S(2)}, u32[]{:S(2)}) collective-permute-start(f32[1,2,64,16]{2,3,1,0:T(8,128)S(1)} %add_bitcast_fusion), channel_id=1, source_target_pairs={{0,256},{256,512},{512,768},{1,257},{257,513},{513,769},{2,258},{2... | collective-permute-start | bytes 24584 | tf_op jit(solution)/shard_map/ppermute | solution.py:19
  8.6 10.3 %collective-permute-start.1 = (f32[1,2,64,16]{2,3,1,0:T(8,128)S(1)}, f32[1,2,64,16]{2,3,1,0:T(8,128)S(1)}, u32[]{:S(2)}, u32[]{:S(2)}) collective-permute-start(f32[1,2,64,16]{2,3,1,0:T(8,128)S(1)} %bitcast.263), channel_id=1, source_target_pairs={{256,0},{512,256},{768,512},{257,1},{513,257},{769,513},{258,2},{5... | collective-permute-start | bytes 24584 | tf_op jit(solution)/shard_map/ppermute | solution.py:22
  13.7 5.2 %copy-start.5 = (f32[16]{0:T(128)S(1)}, f32[16]{0:T(128)}, u32[]{:S(2)}) copy-start(f32[16]{0:T(128)} %param.14) | copy-start | bytes 196
  16.8 23.9 %copy-start.6 = (f32[128]{0:T(128)S(1)}, f32[128]{0:T(128)}, u32[]{:S(2)}) copy-start(f32[128]{0:T(128)} %param.17) | copy-start | bytes 1540
  16.9 38.3 %copy-start.4 = (bf16[64,4608]{1,0:T(8,128)(2,1)S(1)}, bf16[64,4608]{1,0:T(8,128)(2,1)}, u32[]{:S(2)}) copy-start(bf16[64,4608]{1,0:T(8,128)(2,1)} %param.15) | copy-start | bytes 1769476
  20.3 34.5 %all-to-all-start = ((bf16[32,128,64]{1,2,0:T(8,128)(2,1)}), bf16[32,128,64]{1,2,0:T(8,128)(2,1)S(1)}, u32[]{:S(2)}, u32[]{:S(2)}) async-start(bf16[32,128,64]{1,2,0:T(8,128)(2,1)} %broadcast_select_fusion), calls=%async_computation | async-start | bytes 1048576 | tf_op jit(solution)/shard_map/all_to_all | solution.py:147
  55.6 6.4 %copy-start.7 = (f32[128]{0:T(128)S(1)}, f32[128]{0:T(128)}, u32[]{:S(2)}) copy-start(f32[128]{0:T(128)} %param.16) | copy-start | bytes 1540
  58.0 9.8 %all-to-all-start.1 = ((bf16[4,2,128,64]{2,3,1,0:T(8,128)(2,1)}), bf16[4,2,128,64]{2,3,1,0:T(8,128)(2,1)S(1)}, u32[]{:S(2)}, u32[]{:S(2)}) async-start(bf16[4,2,128,64]{2,3,1,0:T(8,128)(2,1)} %broadcast_in_dim.130), calls=%async_computation.1 | async-start | bytes 262144 | tf_op jit(solution)/shard_map/all_to_all | solution.py:35
  117.3 1.4 %copy-start.2 = (bf16[1,512,1536]{1,2,0:T(8,128)(2,1)S(1)}, bf16[1,512,1536]{1,2,0:T(8,128)(2,1)}, u32[]{:S(2)}) copy-start(bf16[1,512,1536]{1,2,0:T(8,128)(2,1)} %copy.217) | copy-start | bytes 4718596
  124.0 1.4 %copy-start.3 = (bf16[1,512,1536]{1,2,0:T(8,128)(2,1)S(1)}, bf16[1,512,1536]{1,2,0:T(8,128)(2,1)}, u32[]{:S(2)}) copy-start(bf16[1,512,1536]{1,2,0:T(8,128)(2,1)} %copy.208) | copy-start | bytes 4718596
  125.4 2.3 %copy-start.1 = (bf16[3,3,3,512,16]{3,4,2,1,0:T(8,128)(2,1)S(1)}, bf16[3,3,3,512,16]{3,4,2,1,0:T(8,128)(2,1)}, u32[]{:S(2)}) copy-start(bf16[3,3,3,512,16]{3,4,2,1,0:T(8,128)(2,1)} %param.13) | copy-start | bytes 1327108
where the time goes:
time: 129 us; the launch traced here: 128 us
  local copies, waits for them, and re-layouts  41.8 us (32%)
  other arithmetic  28.6 us (22%)
  starting transfers between devices  23.2 us (18%)
  waiting for transfers between devices  18 us (14%)
  matrix products  14.5 us (11%)
  between operations  1.54 us (1%)
    all_to_all x1, starting transfers between devices, shards(): lax.all_to_all(outgoing, 'group', split_axis=0, concat_axis=0, tiled=True)  14.4 us
    all_to_all x1, waiting for transfers between devices, shards(): lax.all_to_all(outgoing, 'group', split_axis=0, concat_axis=0, tiled=True)  14 us
    mul x2, local copies, waits for them, and re-layouts, head_norm(): shaped * lax.rsqrt(jnp.mean(shaped * shaped, axis=-1, keepdims=True) + 1e...  9.98 us
    mul x1, local copies, waits for them, and re-layouts, head_norm(): shaped * shaped  6.56 us
    dot_general x1, matrix products, shards(): jnp.einsum('ctf,fe->cte', flat_rows, pair_weight, preferred_element_type=...  6.39 us
    slice x3, local copies, waits for them, and re-layouts, shards(): key_rows = key_values[slot_at, :, :D].reshape(clip_tokens, HEADS, HEAD)  6.39 us
    convert_element_type x1, other arithmetic, shards(): normed = head_norm(projected[..., :D], key_gain, HEAD).reshape(projected....  6.21 us
    mul x1, other arithmetic, head_norm(): shaped * shaped  6.04 us
  transfers between devices with their start and end apart: 4, of which 2 were waited for; matrix products, arithmetic and copies ran while one was open for 13% of the time, Pallas kernels for 0%

commit v1 on v0

v1 whole, which is shorter than its diff:
```python
import math

import jax
import jax.numpy as jnp
from jax import lax
from jax.experimental import pallas as pl
from jax.experimental.pallas import tpu as pltpu
from jax.sharding import PartitionSpec as P

HEADS = 12
HEAD = 128
D = 1536
CAP = 2
N_X = 8
ZC = 16
MESH = pl.DeviceIdType.MESH
STEPS = 3
PER_STEP = HEADS // STEPS


def dot(a, b, dims=((1,), (0,))):
    return lax.dot_general(a, b, (dims, ((), ())), preferred_element_type=jnp.float32)


def route_kernel(feat_hbm, weight_hbm, bias, bucket, out, feat, weight, halo_out, halo_in,
                 xbuf, pick_out, pick_in, ysum, ybuf,
                 load_sem, halo_ssem, halo_rsem, x_ssem, x_rsem, c_ssem, c_rsem, y_ssem, y_rsem):
    tile = lax.axis_index("tile")
    seq = lax.axis_index("seq")
    group = lax.axis_index("group")
    n_tile = lax.axis_size("tile")
    x_at = group // 4
    hi_at = (group // 2) % 2
    core_at = group % 2

    def at_x(step):
        return {"group": ((x_at + step) % N_X) * 4 + hi_at * 2 + core_at}

    def at_y(step_hi, step_tile):
        return {"tile": (tile + step_tile) % n_tile,
                "group": x_at * 4 + ((hi_at + step_hi) % 2) * 2 + core_at}

    partner = {"group": x_at * 4 + hi_at * 2 + (1 - core_at)}
    y_steps = [(1, 0), (1, 1), (1, 3), (1, 2), (0, 2), (0, 1), (0, 3)]

    barrier = pltpu.get_barrier_semaphore()
    for step in (4, 3, 5, 2, 6, 1, 7):
        pl.semaphore_signal(barrier, inc=1, device_id=at_x(step), device_id_type=MESH)
    for step in y_steps:
        pl.semaphore_signal(barrier, inc=1, device_id=at_y(*step), device_id_type=MESH)
    pl.semaphore_signal(barrier, inc=1, device_id=partner, device_id_type=MESH)

    load_weight = pltpu.make_async_copy(weight_hbm, weight, load_sem.at[0])
    load_feat = pltpu.make_async_copy(feat_hbm, feat, load_sem.at[1])
    load_weight.start()
    load_feat.start()
    xbuf[N_X] = jnp.zeros((64, 128), jnp.bfloat16)

    buckets = [x_at * 4 + ((hi_at + d_hi) % 2) * 2 + (core_at + d_core) % 2
               for d_hi in range(2) for d_core in range(2)]

    def scan_slot(g, carry):
        here = bucket[seq, g]
        done = []
        for at, wanted in enumerate(buckets):
            first, second, count = carry[3 * at : 3 * at + 3]
            hit = here == wanted
            first = jnp.where(hit & (count == 0), g, first)
            second = jnp.where(hit & (count == 1), g, second)
            count = count + jnp.where(hit, 1, 0)
            done += [first, second, count]
        return tuple(done)

    slots = lax.fori_loop(0, 32, scan_slot, (jnp.int32(0),) * 12)

    load_weight.wait()
    load_feat.wait()

    taps = weight[...]
    first_frame = feat[0].reshape(256, 512)
    second_frame = feat[1].reshape(256, 512)
    from_first = dot(taps, first_frame, ((1,), (1,)))
    from_second = dot(taps[288:], second_frame, ((1,), (1,)))
    both = from_first[:144] + from_first[144:288]
    frame_sums = (both + from_first[288:], both + from_second)

    lane = lax.broadcasted_iota(jnp.int32, (ZC, 128), 1)
    column = lane % 64
    low_half = lane < 64

    def columns(sums, row_tap, pair):
        def at(col_tap):
            begin = (row_tap * 3 + col_tap) * ZC
            return sums[begin : begin + ZC, pair * 128 : pair * 128 + 128]

        left, middle, right = at(0), at(1), at(2)
        left = jnp.where(column == 0, left, pltpu.roll(left, 1, 1))
        right = jnp.where(column == 63, right, pltpu.roll(right, 127, 1))
        return left + middle + right

    part = [[[columns(frame_sums[f], row_tap, pair) for pair in range(2)]
             for row_tap in range(3)] for f in range(2)]

    def swap(value):
        return pltpu.roll(value, 64, 1)

    up, down = 0, 2
    halo_out[0] = jnp.where(low_half, part[0][down][0], swap(part[1][down][0]))
    halo_out[1] = jnp.where(low_half, swap(part[0][up][1]), part[1][up][1])
    halo_in[0] = jnp.where(low_half, part[0][up][0], swap(part[1][up][0]))
    halo_in[1] = jnp.where(low_half, swap(part[0][down][1]), part[1][down][1])

    pl.semaphore_wait(barrier, 15)

    to_prev = pltpu.make_async_remote_copy(
        src_ref=halo_out.at[0], dst_ref=halo_in.at[3], send_sem=halo_ssem.at[0],
        recv_sem=halo_rsem.at[0], device_id={"tile": (tile + n_tile - 1) % n_tile},
        device_id_type=MESH)
    to_next = pltpu.make_async_remote_copy(
        src_ref=halo_out.at[1], dst_ref=halo_in.at[2], send_sem=halo_ssem.at[1],
        recv_sem=halo_rsem.at[1], device_id={"tile": (tile + 1) % n_tile},
        device_id_type=MESH)
    has_prev = tile > 0
    has_next = tile < n_tile - 1

    @pl.when(has_prev)
    def _():
        to_prev.start()

    @pl.when(has_next)
    def _():
        to_next.start()

    bias_column = jnp.zeros((ZC, 128), jnp.float32)
    channel = lax.broadcasted_iota(jnp.int32, (ZC, 128), 0)
    for k in range(ZC):
        bias_column = jnp.where(channel == k, bias[k], bias_column)

    @pl.when(has_prev)
    def _():
        to_next.wait_recv()

    @pl.when(has_next)
    def _():
        to_prev.wait_recv()

    top = halo_in[jnp.where(has_prev, 2, 0)]
    bottom = halo_in[jnp.where(has_next, 3, 1)]
    latent = []
    for f in range(2):
        top_f = top if f == 0 else swap(top)
        bottom_f = swap(bottom) if f == 0 else bottom
        above = [swap(part[f][up][pair]) for pair in range(2)]
        below = [swap(part[f][down][pair]) for pair in range(2)]
        shifted_up = (jnp.where(low_half, top_f, above[0]), jnp.where(low_half, above[0], above[1]))
        shifted_down = (jnp.where(low_half, below[0], below[1]), jnp.where(low_half, below[1], bottom_f))
        for pair in range(2):
            total = shifted_up[pair] + part[f][1][pair] + shifted_down[pair] + bias_column
            latent.append(total.astype(jnp.bfloat16))

    rows_at = lax.broadcasted_iota(jnp.int32, (128, 128), 0)
    lanes_at = lax.broadcasted_iota(jnp.int32, (128, 128), 1)
    wanted_row = (lanes_at // 64) * 64 + (lanes_at % 32) * 2 + (lanes_at // 32) % 2
    selector = jnp.where(rows_at == wanted_row, 1.0, 0.0).astype(jnp.bfloat16)
    chosen = dot(jnp.concatenate(latent, axis=0), selector)
    block = lane // 32
    patch_rows = []
    for yx in range(4):
        merged = jnp.zeros((ZC, 128), jnp.float32)
        for fi in range(4):
            piece = chosen[fi * ZC : fi * ZC + ZC]
            if fi != yx:
                piece = pltpu.roll(piece, ((fi - yx) % 4) * 32, 1)
            merged = jnp.where(block == fi, piece, merged)
        patch_rows.append(merged)
    xbuf[0] = jnp.concatenate(patch_rows, axis=0).astype(jnp.bfloat16)

    x_copies = []
    for step in (4, 3, 5, 2, 6, 1, 7):
        copy = pltpu.make_async_remote_copy(
            src_ref=xbuf.at[0], dst_ref=xbuf.at[step], send_sem=x_ssem.at[step],
            recv_sem=x_rsem.at[step], device_id=at_x(step), device_id_type=MESH)
        copy.start()
        x_copies.append(copy)

    picks = []
    for at in range(4):
        first, second, count = slots[3 * at : 3 * at + 3]
        for slot, source in enumerate((first, second)):
            mine = (count > slot) & (source % 4 == hi_at * 2 + core_at)
            picks.append(jnp.where(mine, (x_at + N_X - source // 4) % N_X, N_X))

    for copy in x_copies:
        copy.wait_recv()

    for d_hi in range(2):
        for slot in range(CAP):
            pick_out[d_hi, slot] = xbuf[picks[(d_hi * 2 + 1) * 2 + slot]]
    across = pltpu.make_async_remote_copy(
        src_ref=pick_out, dst_ref=pick_in, send_sem=c_ssem.at[0], recv_sem=c_rsem.at[0],
        device_id=partner, device_id_type=MESH)
    across.start()
    own = [[xbuf[picks[d_hi * 4 + slot]] for slot in range(CAP)] for d_hi in range(2)]
    across.wait_recv()
    for d_hi in range(2):
        for slot in range(CAP):
            ysum[d_hi, slot] = own[d_hi][slot] + pick_in[d_hi, slot]

    y_copies = []
    for d_hi, d_tile in y_steps:
        at = d_hi * 4 + d_tile
        copy = pltpu.make_async_remote_copy(
            src_ref=ysum.at[d_hi], dst_ref=ybuf.at[at], send_sem=y_ssem.at[at],
            recv_sem=y_rsem.at[at], device_id=at_y(d_hi, d_tile), device_id_type=MESH)
        copy.start()
        y_copies.append(copy)
    for copy in y_copies:
        copy.wait_recv()
    for slot in range(CAP):
        for d_tile in range(4):
            own_side = ysum[0, slot] if d_tile == 0 else ybuf[d_tile, slot]
            out[slot, d_tile] = own_side + ybuf[4 + d_tile, slot]

    @pl.when(has_prev)
    def _():
        to_prev.wait_send()

    @pl.when(has_next)
    def _():
        to_next.wait_send()

    for copy in x_copies:
        copy.wait_send()
    across.wait_send()
    for copy in y_copies:
        copy.wait_send()


def route(features, taps, bias, bucket):
    return pl.pallas_call(
        route_kernel,
        out_shape=jax.ShapeDtypeStruct((CAP, 4, 64, 128), jnp.bfloat16),
        in_specs=[
            pl.BlockSpec(memory_space=pl.ANY),
            pl.BlockSpec(memory_space=pl.ANY),
            pl.BlockSpec(memory_space=pltpu.SMEM),
            pl.BlockSpec(memory_space=pltpu.SMEM),
        ],
        out_specs=pl.BlockSpec(memory_space=pltpu.VMEM),
        scratch_shapes=[
            pltpu.VMEM((2, 4, 64, 512), jnp.bfloat16),
            pltpu.VMEM((432, 512), jnp.bfloat16),
            pltpu.VMEM((2, ZC, 128), jnp.float32),
            pltpu.VMEM((4, ZC, 128), jnp.float32),
            pltpu.VMEM((N_X + 1, 64, 128), jnp.bfloat16),
            pltpu.VMEM((2, CAP, 64, 128), jnp.bfloat16),
            pltpu.VMEM((2, CAP, 64, 128), jnp.bfloat16),
            pltpu.VMEM((2, CAP, 64, 128), jnp.bfloat16),
            pltpu.VMEM((8, CAP, 64, 128), jnp.bfloat16),
            pltpu.SemaphoreType.DMA((2,)),
            pltpu.SemaphoreType.DMA((2,)),
            pltpu.SemaphoreType.DMA((2,)),
            pltpu.SemaphoreType.DMA((N_X,)),
            pltpu.SemaphoreType.DMA((N_X,)),
            pltpu.SemaphoreType.DMA((1,)),
            pltpu.SemaphoreType.DMA((1,)),
            pltpu.SemaphoreType.DMA((8,)),
            pltpu.SemaphoreType.DMA((8,)),
        ],
        compiler_params=pltpu.CompilerParams(collective_id=0, has_side_effects=True),
        name="route",
    )(features, taps, bias, bucket)


def attend_kernel(patches, weight, query_gain, key_gain, bucket, frames, out, flat, tall, ones):
    step = pl.program_id(0)
    seq = lax.axis_index("seq")
    group = lax.axis_index("group")

    def scan_slot(g, carry):
        first, second, count = carry
        hit = bucket[seq, g] == group
        total = frames[seq, g]
        first = jnp.where(hit & (count == 0), total, first)
        second = jnp.where(hit & (count == 1), total, second)
        return first, second, count + jnp.where(hit, 1, 0)

    zero = jnp.int32(0)
    slot_frames = lax.fori_loop(0, 32, scan_slot, (zero, zero, zero))[:2]

    @pl.when(step == 0)
    def _():
        token = lax.broadcasted_iota(jnp.int32, (512, 128), 0)
        for slot in range(CAP):
            valid = (token % 128) // 64 < slot_frames[slot]
            ones[slot] = jnp.where(valid, 1.0, 0.0).astype(jnp.bfloat16)
            for at in range(4):
                piece = patches[slot, at]
                flat[slot, :, at * 128 : at * 128 + 128] = piece
                upright = piece.astype(jnp.float32).T
                keep = valid[:128, :64]
                tall[0, slot, at * 128 : at * 128 + 128] = upright.astype(jnp.bfloat16)
                tall[1, slot, at * 128 : at * 128 + 128] = jnp.where(keep, upright, 0.0).astype(jnp.bfloat16)

    gain = query_gain[...] * key_gain[...] * (math.log2(math.e) / math.sqrt(HEAD))
    query_token = lax.broadcasted_iota(jnp.int32, (128, HEAD), 0)
    for slot in range(CAP):
        keep = query_token // 64 < slot_frames[slot]
        rows = tall[0, slot, :128]
        valid_rows = tall[1, slot]
        across = flat[slot]
        for local in range(PER_STEP):
            begin = local * HEAD
            head_at = pl.multiple_of(step * (PER_STEP * HEAD) + begin, HEAD)
            query_weight = weight[:, pl.ds(head_at, HEAD)]
            key_weight = weight[:, pl.ds(pl.multiple_of(head_at + D, HEAD), HEAD)]
            value_weight = weight[:, pl.ds(pl.multiple_of(head_at + 2 * D, HEAD), HEAD)]
            u = dot(rows, query_weight)
            mean = jnp.mean(u * u, axis=1, keepdims=True)
            q = (u * lax.rsqrt(mean + 1e-6) * gain).astype(jnp.bfloat16)
            u = dot(key_weight, across, ((0,), (0,)))
            mean = jnp.mean(u * u, axis=0, keepdims=True)
            k = (u * lax.rsqrt(mean + 1e-6)).astype(jnp.bfloat16)
            v = dot(valid_rows, value_weight).astype(jnp.bfloat16)
            weights = jnp.exp2(dot(q, k)).astype(jnp.bfloat16)
            mixed = dot(weights, jnp.concatenate([v, ones[slot]], axis=1))
            result = mixed[:, :HEAD] / mixed[:, HEAD:]
            out[0, 0, slot, :, begin : begin + HEAD] = jnp.where(keep, result, 0.0).astype(jnp.bfloat16)


def attend(patches, weight, query_gain, key_gain, bucket, frames):
    whole = pl.BlockSpec(memory_space=pltpu.VMEM)
    return pl.pallas_call(
        attend_kernel,
        grid=(STEPS,),
        out_shape=jax.ShapeDtypeStruct((1, 1, CAP, 128, D), jnp.bfloat16),
        in_specs=[
            whole, whole, whole, whole,
            pl.BlockSpec(memory_space=pltpu.SMEM),
            pl.BlockSpec(memory_space=pltpu.SMEM),
        ],
        out_specs=pl.BlockSpec((1, 1, CAP, 128, PER_STEP * HEAD), lambda i: (0, 0, 0, 0, i)),
        scratch_shapes=[
            pltpu.VMEM((CAP, 64, 512), jnp.bfloat16),
            pltpu.VMEM((2, CAP, 512, 64), jnp.bfloat16),
            pltpu.VMEM((CAP, 512, 128), jnp.bfloat16),
        ],
        name="attend",
    )(patches, weight, query_gain, key_gain, bucket, frames)


def shards(features, conv_weight, conv_bias, embed_qkv, query_gain, key_gain, bucket, frames):
    taps = jnp.transpose(conv_weight, (0, 1, 2, 4, 3)).reshape(432, 512)
    patches = route(features[0, 0], taps, conv_bias, bucket)
    return attend(
        patches, embed_qkv, query_gain.reshape(1, HEAD), key_gain.reshape(1, HEAD), bucket, frames
    )


def solution(mesh):
    in_specs = (P("seq", "group", None, "tile", None, None), P(), P(), P(), P(), P(), P(), P())
    out_specs = P("seq", "group", None, "tile", None)
    return jax.shard_map(shards, mesh=mesh, in_specs=in_specs, out_specs=out_specs, check_vma=False)
```

time: 129 us -> 44.4 us (0.34)
  the two profiles are of different devices: /device:TPU:2 before, /device:TPU:3 now
where the time goes in v1:
time: 44.4 us; the launch traced here: 44.1 us
  Pallas kernels  44.1 us (99%)
    pallas_call x1, Pallas kernels, route(): pl.pallas_call(route_kernel, out_shape=jax.ShapeDtypeStruct((CAP, 4, 64,...  32.2 us
    pallas_call x1, Pallas kernels, attend(): pl.pallas_call(attend_kernel, grid=(STEPS,), out_shape=jax.ShapeDtypeStru...  11.9 us

profile of v1, /device:TPU:3, one launch (start us, length us, event | category | flops | bytes accessed | tf_op | source)
XLA Modules:
  0.0 44.1 jit_solution(437878566013766989)
XLA Ops:
  0.0 32.2 %route.1.patches = bf16[2,4,64,128]{3,2,1,0:T(8,128)(2,1)} custom-call(bf16[2,4,64,512]{3,2,1,0:T(8,128)(2,1)} %bitcast.6, bf16[432,512]{1,0:T(8,128)(2,1)} %bitcast.7, f32[16]{0:T(128)} %bias.1, s32[8,32]{1,0:T(8,128)} %bucket.3), custom_call_target="tpu_custom_call" | custom-call | tf_op jit(solution)/shard_map/route/pallas_call | solution.py:240
  32.2 11.9 %attend.1 = bf16[1,1,2,128,1536]{4,3,2,1,0:T(8,128)(2,1)} custom-call(bf16[2,4,64,128]{3,2,1,0:T(8,128)(2,1)} %route.1.patches, bf16[64,4608]{1,0:T(8,128)(2,1)} %weight.1, f32[1,128]{1,0:T(1,128)} %bitcast.8, f32[1,128]{1,0:T(1,128)} %bitcast.9, s32[8,32]{1,0:T(8,128)} %bucket.3, s32[8,32]{1,0:T(8,128)} %frames.1), custom_call_target="tpu_custom_call" | custom-call | tf_op jit(solution)/shard_map/attend/pallas_call | solution.py:333

commit v2 on v1

v2 whole, which is shorter than its diff:
```python
import math

import jax
import jax.numpy as jnp
from jax import lax
from jax.experimental import pallas as pl
from jax.experimental.pallas import tpu as pltpu
from jax.sharding import PartitionSpec as P

HEADS = 12
HEAD = 128
D = 1536
CAP = 2
N_X = 8
ZC = 16
MESH = pl.DeviceIdType.MESH


def dot(a, b, dims=((1,), (0,))):
    return lax.dot_general(a, b, (dims, ((), ())), preferred_element_type=jnp.float32)


def fused_kernel(feat_hbm, taps_hbm, bias_hbm, embed_hbm, query_gain, key_gain, bucket_hbm,
                 frames_hbm, out_hbm,
                 feat, taps_ref, bias, embed, bucket, frames, key_rows, halo_out, halo_in,
                 xbuf, pick_out, pick_in, ysum, ybuf, queries, keys, values, ones, soft, result,
                 load_sem, halo_ssem, halo_rsem, x_ssem, x_rsem, c_ssem, c_rsem, y_ssem, y_rsem,
                 out_sem):
    tile = lax.axis_index("tile")
    seq = lax.axis_index("seq")
    group = lax.axis_index("group")
    n_tile = lax.axis_size("tile")
    x_at = group // 4
    hi_at = (group // 2) % 2
    core_at = group % 2

    def at_x(step):
        return {"group": ((x_at + step) % N_X) * 4 + hi_at * 2 + core_at}

    def at_y(step_hi, step_tile):
        return {"tile": (tile + step_tile) % n_tile,
                "group": x_at * 4 + ((hi_at + step_hi) % 2) * 2 + core_at}

    partner = {"group": x_at * 4 + hi_at * 2 + (1 - core_at)}
    y_steps = [(1, 0), (1, 1), (1, 3), (1, 2), (0, 2), (0, 1), (0, 3)]

    loads = [
        pltpu.make_async_copy(source, target, load_sem.at[at])
        for at, (source, target) in enumerate((
            (taps_hbm, taps_ref), (feat_hbm, feat), (bias_hbm, bias), (bucket_hbm, bucket),
            (frames_hbm, frames), (embed_hbm, embed)))
    ]
    for load in loads:
        load.start()

    barrier = pltpu.get_barrier_semaphore()
    for step in (4, 3, 5, 2, 6, 1, 7):
        pl.semaphore_signal(barrier, inc=1, device_id=at_x(step), device_id_type=MESH)
    for step in y_steps:
        pl.semaphore_signal(barrier, inc=1, device_id=at_y(*step), device_id_type=MESH)
    pl.semaphore_signal(barrier, inc=1, device_id=partner, device_id_type=MESH)

    xbuf[N_X] = jnp.zeros((64, 128), jnp.bfloat16)
    for load in loads[:2]:
        load.wait()
    taps = taps_ref[...]
    first_frame = feat[0].reshape(256, 512)
    second_frame = feat[1].reshape(256, 512)
    from_first = dot(taps, first_frame, ((1,), (1,)))
    from_second = dot(taps[288:], second_frame, ((1,), (1,)))
    both = from_first[:144] + from_first[144:288]
    frame_sums = (both + from_first[288:], both + from_second)

    lane = lax.broadcasted_iota(jnp.int32, (ZC, 128), 1)
    column = lane % 64
    low_half = lane < 64

    def columns(sums, row_tap, pair):
        def at(col_tap):
            begin = (row_tap * 3 + col_tap) * ZC
            return sums[begin : begin + ZC, pair * 128 : pair * 128 + 128]

        left, middle, right = at(0), at(1), at(2)
        left = jnp.where(column == 0, left, pltpu.roll(left, 1, 1))
        right = jnp.where(column == 63, right, pltpu.roll(right, 127, 1))
        return left + middle + right

    part = [[[columns(frame_sums[f], row_tap, pair) for pair in range(2)]
             for row_tap in range(3)] for f in range(2)]

    def swap(value):
        return pltpu.roll(value, 64, 1)

    up, down = 0, 2
    halo_out[0] = jnp.where(low_half, part[0][down][0], swap(part[1][down][0]))
    halo_out[1] = jnp.where(low_half, swap(part[0][up][1]), part[1][up][1])
    halo_in[0] = jnp.where(low_half, part[0][up][0], swap(part[1][up][0]))
    halo_in[1] = jnp.where(low_half, swap(part[0][down][1]), part[1][down][1])

    pl.semaphore_wait(barrier, 15)

    to_prev = pltpu.make_async_remote_copy(
        src_ref=halo_out.at[0], dst_ref=halo_in.at[3], send_sem=halo_ssem.at[0],
        recv_sem=halo_rsem.at[0], device_id={"tile": (tile + n_tile - 1) % n_tile},
        device_id_type=MESH)
    to_next = pltpu.make_async_remote_copy(
        src_ref=halo_out.at[1], dst_ref=halo_in.at[2], send_sem=halo_ssem.at[1],
        recv_sem=halo_rsem.at[1], device_id={"tile": (tile + 1) % n_tile},
        device_id_type=MESH)
    has_prev = tile > 0
    has_next = tile < n_tile - 1

    @pl.when(has_prev)
    def _():
        to_prev.start()

    @pl.when(has_next)
    def _():
        to_next.start()

    for load in loads[2:5]:
        load.wait()
    buckets = [x_at * 4 + ((hi_at + d_hi) % 2) * 2 + (core_at + d_core) % 2
               for d_hi in range(2) for d_core in range(2)]

    def scan_slot(g, carry):
        here = bucket[seq, g]
        done = []
        for at, wanted in enumerate(buckets):
            first, second, count = carry[3 * at : 3 * at + 3]
            hit = here == wanted
            first = jnp.where(hit & (count == 0), g, first)
            second = jnp.where(hit & (count == 1), g, second)
            count = count + jnp.where(hit, 1, 0)
            done += [first, second, count]
        return tuple(done)

    slots = lax.fori_loop(0, 32, scan_slot, (jnp.int32(0),) * 12)

    bias_column = jnp.zeros((ZC, 128), jnp.float32)
    channel = lax.broadcasted_iota(jnp.int32, (ZC, 128), 0)
    for k in range(ZC):
        bias_column = jnp.where(channel == k, bias[k], bias_column)

    @pl.when(has_prev)
    def _():
        to_next.wait_recv()

    @pl.when(has_next)
    def _():
        to_prev.wait_recv()

    top = halo_in[jnp.where(has_prev, 2, 0)]
    bottom = halo_in[jnp.where(has_next, 3, 1)]
    latent = []
    for f in range(2):
        top_f = top if f == 0 else swap(top)
        bottom_f = swap(bottom) if f == 0 else bottom
        above = [swap(part[f][up][pair]) for pair in range(2)]
        below = [swap(part[f][down][pair]) for pair in range(2)]
        shifted_up = (jnp.where(low_half, top_f, above[0]), jnp.where(low_half, above[0], above[1]))
        shifted_down = (jnp.where(low_half, below[0], below[1]), jnp.where(low_half, below[1], bottom_f))
        for pair in range(2):
            total = shifted_up[pair] + part[f][1][pair] + shifted_down[pair] + bias_column
            latent.append(total.astype(jnp.bfloat16))

    rows_at = lax.broadcasted_iota(jnp.int32, (128, 128), 0)
    lanes_at = lax.broadcasted_iota(jnp.int32, (128, 128), 1)
    wanted_row = (lanes_at // 64) * 64 + (lanes_at % 32) * 2 + (lanes_at // 32) % 2
    selector = jnp.where(rows_at == wanted_row, 1.0, 0.0).astype(jnp.bfloat16)
    chosen = dot(jnp.concatenate(latent, axis=0), selector)
    block = lane // 32
    patch_rows = []
    for yx in range(4):
        merged = jnp.zeros((ZC, 128), jnp.float32)
        for fi in range(4):
            piece = chosen[fi * ZC : fi * ZC + ZC]
            if fi != yx:
                piece = pltpu.roll(piece, ((fi - yx) % 4) * 32, 1)
            merged = jnp.where(block == fi, piece, merged)
        patch_rows.append(merged)
    xbuf[0] = jnp.concatenate(patch_rows, axis=0).astype(jnp.bfloat16)

    x_copies = []
    for step in (4, 3, 5, 2, 6, 1, 7):
        copy = pltpu.make_async_remote_copy(
            src_ref=xbuf.at[0], dst_ref=xbuf.at[step], send_sem=x_ssem.at[step],
            recv_sem=x_rsem.at[step], device_id=at_x(step), device_id_type=MESH)
        copy.start()
        x_copies.append(copy)

    picks = []
    for at in range(4):
        first, second, count = slots[3 * at : 3 * at + 3]
        for slot, source in enumerate((first, second)):
            mine = (count > slot) & (source % 4 == hi_at * 2 + core_at)
            picks.append(jnp.where(mine, (x_at + N_X - source // 4) % N_X, N_X))

    loads[5].wait()
    for at in range(HEADS):
        piece = embed[:, D + at * HEAD : D + at * HEAD + HEAD]
        key_rows[at * HEAD : at * HEAD + HEAD] = piece.astype(jnp.float32).T.astype(jnp.bfloat16)
    gain = query_gain[...] * key_gain[...] * (math.log2(math.e) / math.sqrt(HEAD))
    token = lax.broadcasted_iota(jnp.int32, (128, HEAD), 0)
    valid = []
    for slot in range(CAP):
        first, second, count = slots[:3]
        total = jnp.where(count > slot, frames[seq, second if slot else first], 0)
        keep = token // 64 < total
        valid.append(keep)
        ones[slot] = jnp.where(keep, 1.0, 0.0).astype(jnp.bfloat16)

    for copy in x_copies:
        copy.wait_recv()

    for d_hi in range(2):
        for slot in range(CAP):
            pick_out[d_hi, slot] = xbuf[picks[(d_hi * 2 + 1) * 2 + slot]]
    across = pltpu.make_async_remote_copy(
        src_ref=pick_out, dst_ref=pick_in, send_sem=c_ssem.at[0], recv_sem=c_rsem.at[0],
        device_id=partner, device_id_type=MESH)
    across.start()
    own = [[xbuf[picks[d_hi * 4 + slot]] for slot in range(CAP)] for d_hi in range(2)]
    across.wait_recv()
    for d_hi in range(2):
        for slot in range(CAP):
            ysum[d_hi, slot] = own[d_hi][slot] + pick_in[d_hi, slot]

    y_copies = []
    for d_hi, d_tile in y_steps:
        at = d_hi * 4 + d_tile
        copy = pltpu.make_async_remote_copy(
            src_ref=ysum.at[d_hi], dst_ref=ybuf.at[at], send_sem=y_ssem.at[at],
            recv_sem=y_rsem.at[at], device_id=at_y(d_hi, d_tile), device_id_type=MESH)
        copy.start()
        y_copies.append(copy)
    arrivals = {step: copy for step, copy in zip(y_steps, y_copies)}
    for d_tile in range(4):
        arrivals[1, d_tile].wait_recv()
        if d_tile:
            arrivals[0, d_tile].wait_recv()
        near = ysum if d_tile == 0 else ybuf
        parts = [near[d_tile, slot] + ybuf[4 + d_tile, slot] for slot in range(CAP)]
        upright = [parts[slot].astype(jnp.float32).T for slot in range(CAP)]
        if d_tile == 0:
            for slot in range(CAP):
                u = dot(upright[slot].astype(jnp.bfloat16), embed[:, :D])
                for at in range(HEADS):
                    mine = u[:, at * HEAD : at * HEAD + HEAD]
                    mean = jnp.mean(mine * mine, axis=1, keepdims=True)
                    queries[slot, at] = (mine * lax.rsqrt(mean + 1e-6) * gain).astype(jnp.bfloat16)
        joined = jnp.concatenate(parts, axis=1)
        for at in range(HEADS):
            u = dot(key_rows[at * HEAD : at * HEAD + HEAD], joined)
            mean = jnp.mean(u * u, axis=0, keepdims=True)
            keys[d_tile, at] = (u * lax.rsqrt(mean + 1e-6)).astype(jnp.bfloat16)
        tall = jnp.concatenate(
            [jnp.where(valid[slot][:, :64], upright[slot], 0.0) for slot in range(CAP)], axis=0
        ).astype(jnp.bfloat16)
        for at in range(0, HEADS, 2):
            begin = 2 * D + at * HEAD
            v = dot(tall, embed[:, begin : begin + 2 * HEAD]).astype(jnp.bfloat16)
            values[d_tile, at] = v[:, :HEAD]
            values[d_tile, at + 1] = v[:, HEAD:]

    units = [(at, slot) for at in range(HEADS) for slot in range(CAP)]
    out_copies = []
    for turn in range(len(units) + 1):
        if turn < len(units):
            at, slot = units[turn]
            begin = slot * HEAD
            k = jnp.concatenate(
                [keys[part, at, :, begin : begin + HEAD] for part in range(4)], axis=1)
            soft[turn % 3] = jnp.exp2(dot(queries[slot, at], k)).astype(jnp.bfloat16)
        if turn:
            at, slot = units[turn - 1]
            begin = slot * HEAD
            v = jnp.concatenate(
                [jnp.concatenate([values[part, at, begin : begin + HEAD], ones[slot]], axis=1)
                 for part in range(4)], axis=0)
            mixed = dot(soft[(turn - 1) % 3], v)
            final = jnp.where(valid[slot], mixed[:, :HEAD] / mixed[:, HEAD:], 0.0)
            result[slot, :, at * HEAD : at * HEAD + HEAD] = final.astype(jnp.bfloat16)
            if slot == CAP - 1 and at % 3 == 2:
                spot = pl.ds((at - 2) * HEAD, 3 * HEAD)
                copy = pltpu.make_async_copy(
                    result.at[:, :, spot], out_hbm.at[0, 0, :, :, spot], out_sem.at[at // 3])
                copy.start()
                out_copies.append(copy)
    for copy in out_copies:
        copy.wait()

    @pl.when(has_prev)
    def _():
        to_prev.wait_send()

    @pl.when(has_next)
    def _():
        to_next.wait_send()

    for copy in x_copies:
        copy.wait_send()
    across.wait_send()
    for copy in y_copies:
        copy.wait_send()


def fused(features, taps, bias, embed, query_gain, key_gain, bucket, frames):
    anywhere = pl.BlockSpec(memory_space=pl.ANY)
    vector = pl.BlockSpec(memory_space=pltpu.VMEM)
    return pl.pallas_call(
        fused_kernel,
        out_shape=jax.ShapeDtypeStruct((1, 1, CAP, 128, D), jnp.bfloat16),
        in_specs=[anywhere, anywhere, anywhere, anywhere, vector, vector, anywhere, anywhere],
        out_specs=anywhere,
        scratch_shapes=[
            pltpu.VMEM((2, 4, 64, 512), jnp.bfloat16),
            pltpu.VMEM((432, 512), jnp.bfloat16),
            pltpu.SMEM((ZC,), jnp.float32),
            pltpu.VMEM((64, 3 * D), jnp.bfloat16),
            pltpu.SMEM((8, 32), jnp.int32),
            pltpu.SMEM((8, 32), jnp.int32),
            pltpu.VMEM((D, 64), jnp.bfloat16),
            pltpu.VMEM((2, ZC, 128), jnp.float32),
            pltpu.VMEM((4, ZC, 128), jnp.float32),
            pltpu.VMEM((N_X + 1, 64, 128), jnp.bfloat16),
            pltpu.VMEM((2, CAP, 64, 128), jnp.bfloat16),
            pltpu.VMEM((2, CAP, 64, 128), jnp.bfloat16),
            pltpu.VMEM((2, CAP, 64, 128), jnp.bfloat16),
            pltpu.VMEM((8, CAP, 64, 128), jnp.bfloat16),
            pltpu.VMEM((CAP, HEADS, 128, HEAD), jnp.bfloat16),
            pltpu.VMEM((4, HEADS, HEAD, CAP * 128), jnp.bfloat16),
            pltpu.VMEM((4, HEADS, CAP * 128, HEAD), jnp.bfloat16),
            pltpu.VMEM((CAP, 128, HEAD), jnp.bfloat16),
            pltpu.VMEM((3, 128, 512), jnp.bfloat16),
            pltpu.VMEM((CAP, 128, D), jnp.bfloat16),
            pltpu.SemaphoreType.DMA((6,)),
            pltpu.SemaphoreType.DMA((2,)),
            pltpu.SemaphoreType.DMA((2,)),
            pltpu.SemaphoreType.DMA((N_X,)),
            pltpu.SemaphoreType.DMA((N_X,)),
            pltpu.SemaphoreType.DMA((1,)),
            pltpu.SemaphoreType.DMA((1,)),
            pltpu.SemaphoreType.DMA((8,)),
            pltpu.SemaphoreType.DMA((8,)),
            pltpu.SemaphoreType.DMA((4,)),
        ],
        compiler_params=pltpu.CompilerParams(collective_id=0, has_side_effects=True),
        name="fused",
    )(features, taps, bias, embed, query_gain, key_gain, bucket, frames)


def shards(features, conv_weight, conv_bias, embed_qkv, query_gain, key_gain, bucket, frames):
    taps = jnp.transpose(conv_weight, (0, 1, 2, 4, 3)).reshape(432, 512)
    return fused(
        features[0, 0], taps, conv_bias, embed_qkv, query_gain.reshape(1, HEAD),
        key_gain.reshape(1, HEAD), bucket, frames
    )


def solution(mesh):
    in_specs = (P("seq", "group", None, "tile", None, None), P(), P(), P(), P(), P(), P(), P())
    out_specs = P("seq", "group", None, "tile", None)
    return jax.shard_map(shards, mesh=mesh, in_specs=in_specs, out_specs=out_specs, check_vma=False)
```

time: 44.4 us -> 37.6 us (0.85)
  Pallas kernels: 44.1 us -> 35.3 us
  local copies, waits for them, and re-layouts: 0 us -> 2.06 us
    pallas_call x2 -> x1, Pallas kernels: 44.1 us -> 35.3 us  [fused(): pl.pallas_call(fused_kernel, out_shape=jax.ShapeDtypeStruct((1, 1, CAP, 1...]
    unnamed x0 -> x1, local copies, waits for them, and re-layouts: none -> 2.06 us
where the time goes in v2:
time: 37.6 us; the launch traced here: 37.4 us
  Pallas kernels  35.3 us (94%)
  local copies, waits for them, and re-layouts  2.06 us (5%)
    pallas_call x1, Pallas kernels, fused(): pl.pallas_call(fused_kernel, out_shape=jax.ShapeDtypeStruct((1, 1, CAP, 1...  35.3 us
    unnamed x1, local copies, waits for them, and re-layouts  2.06 us

profile of v2, /device:TPU:3, one launch (start us, length us, event | category | flops | bytes accessed | tf_op | source)
XLA Modules:
  0.0 37.4 jit_solution(17543411642763269913)
XLA Ops:
  0.0 35.3 %fused.1 = bf16[1,1,2,128,1536]{4,3,2,1,0:T(8,128)(2,1)} custom-call(bf16[2,4,64,512]{3,2,1,0:T(8,128)(2,1)} %bitcast.6, bf16[432,512]{1,0:T(8,128)(2,1)} %bitcast.7, f32[16]{0:T(128)} %bias_hbm.1, bf16[64,4608]{1,0:T(8,128)(2,1)} %embed_hbm.1, f32[1,128]{1,0:T(1,128)} %bitcast.8, f32[1,128]{1,0:T(1,128)} %bitcast.9, s32[8,32]{1,0:T(8,128)} %bucket_hbm.1, ...), custom_call_target="tpu_custom_call" | custom-call | tf_op jit(solution)/shard_map/fused/pallas_call | solution.py:311
  35.3 2.1 %copy.10 = bf16[1,1,2,128,1536]{4,3,2,1,0:T(8,128)(2,1)} copy(bf16[1,1,2,128,1536]{4,3,2,1,0:T(8,128)(2,1)} %fused.1) | data formatting | bytes 1572864

commit v3 on v2

--- a/solution.py
+++ b/solution.py
@@ -1,3 +1,4 @@
+import functools
 import math
 
 import jax
@@ -21,11 +22,10 @@
 
 
 def fused_kernel(feat_hbm, taps_hbm, bias_hbm, embed_hbm, query_gain, key_gain, bucket_hbm,
-                 frames_hbm, out_hbm,
-                 feat, taps_ref, bias, embed, bucket, frames, key_rows, halo_out, halo_in,
-                 xbuf, pick_out, pick_in, ysum, ybuf, queries, keys, values, ones, soft, result,
-                 load_sem, halo_ssem, halo_rsem, x_ssem, x_rsem, c_ssem, c_rsem, y_ssem, y_rsem,
-                 out_sem):
+                 frames_hbm, result,
+                 feat, taps_ref, bias, embed, gains, bucket, frames, key_rows, halo_out, halo_in,
+                 xbuf, pick_out, pick_in, ysum, ybuf, part_now, queries, keys, values, ones, soft,
+                 load_sem, halo_ssem, halo_rsem, x_ssem, x_rsem, c_ssem, c_rsem, y_ssem, y_rsem):
     tile = lax.axis_index("tile")
     seq = lax.axis_index("seq")
     group = lax.axis_index("group")
@@ -42,24 +42,24 @@
                 "group": x_at * 4 + ((hi_at + step_hi) % 2) * 2 + core_at}
 
     partner = {"group": x_at * 4 + hi_at * 2 + (1 - core_at)}
+    x_steps = (4, 3, 5, 2, 6, 1, 7)
     y_steps = [(1, 0), (1, 1), (1, 3), (1, 2), (0, 2), (0, 1), (0, 3)]
 
     loads = [
         pltpu.make_async_copy(source, target, load_sem.at[at])
         for at, (source, target) in enumerate((
             (taps_hbm, taps_ref), (feat_hbm, feat), (bias_hbm, bias), (bucket_hbm, bucket),
-            (frames_hbm, frames), (embed_hbm, embed)))
+            (frames_hbm, frames), (embed_hbm, embed), (query_gain, gains.at[0]),
+            (key_gain, gains.at[1])))
     ]
     for load in loads:
         load.start()
-
     barrier = pltpu.get_barrier_semaphore()
-    for step in (4, 3, 5, 2, 6, 1, 7):
+    for step in x_steps:
         pl.semaphore_signal(barrier, inc=1, device_id=at_x(step), device_id_type=MESH)
     for step in y_steps:
         pl.semaphore_signal(barrier, inc=1, device_id=at_y(*step), device_id_type=MESH)
     pl.semaphore_signal(barrier, inc=1, device_id=partner, device_id_type=MESH)
-
     xbuf[N_X] = jnp.zeros((64, 128), jnp.bfloat16)
     for load in loads[:2]:
         load.wait()
@@ -196,11 +196,12 @@
             mine = (count > slot) & (source % 4 == hi_at * 2 + core_at)
             picks.append(jnp.where(mine, (x_at + N_X - source // 4) % N_X, N_X))
 
-    loads[5].wait()
+    for load in loads[5:]:
+        load.wait()
     for at in range(HEADS):
         piece = embed[:, D + at * HEAD : D + at * HEAD + HEAD]
         key_rows[at * HEAD : at * HEAD + HEAD] = piece.astype(jnp.float32).T.astype(jnp.bfloat16)
-    gain = query_gain[...] * key_gain[...] * (math.log2(math.e) / math.sqrt(HEAD))
+    gain = gains[0] * gains[1] * (math.log2(math.e) / math.sqrt(HEAD))
     token = lax.broadcasted_iota(jnp.int32, (128, HEAD), 0)
     valid = []
     for slot in range(CAP):
@@ -235,36 +236,47 @@
         copy.start()
         y_copies.append(copy)
     arrivals = {step: copy for step, copy in zip(y_steps, y_copies)}
-    for d_tile in range(4):
+    turns = ((2, 3, 0, 1), (2, 3, 1, 0), (2, 3, 0, 1), (2, 3, 0, 1))
+
+    def take(d_tile):
         arrivals[1, d_tile].wait_recv()
         if d_tile:
             arrivals[0, d_tile].wait_recv()
-        near = ysum if d_tile == 0 else ybuf
-        parts = [near[d_tile, slot] + ybuf[4 + d_tile, slot] for slot in range(CAP)]
-        upright = [parts[slot].astype(jnp.float32).T for slot in range(CAP)]
-        if d_tile == 0:
-            for slot in range(CAP):
-                u = dot(upright[slot].astype(jnp.bfloat16), embed[:, :D])
-                for at in range(HEADS):
-                    mine = u[:, at * HEAD : at * HEAD + HEAD]
-                    mean = jnp.mean(mine * mine, axis=1, keepdims=True)
-                    queries[slot, at] = (mine * lax.rsqrt(mean + 1e-6) * gain).astype(jnp.bfloat16)
+        near = ybuf if d_tile else ysum
+        for slot in range(CAP):
+            part_now[slot] = near[d_tile, slot] + ybuf[4 + d_tile, slot]
+
+    def make_queries():
+        for slot in range(CAP):
+            u = dot(part_now[slot].astype(jnp.float32).T.astype(jnp.bfloat16), embed[:, :D])
+            for at in range(HEADS):
+                mine = u[:, at * HEAD : at * HEAD + HEAD]
+                mean = jnp.mean(mine * mine, axis=1, keepdims=True)
+                queries[slot, at] = (mine * lax.rsqrt(mean + 1e-6) * gain).astype(jnp.bfloat16)
+
+    for turn in range(4):
+        for here in range(4):
+            pl.when(tile == here)(functools.partial(take, (here - turns[here][turn]) % 4))
+        own_turn = {0: tile == 2, 1: tile == 3, 2: tile < 2}
+        if turn in own_turn:
+            pl.when(own_turn[turn])(make_queries)
+        parts = [part_now[slot] for slot in range(CAP)]
         joined = jnp.concatenate(parts, axis=1)
         for at in range(HEADS):
             u = dot(key_rows[at * HEAD : at * HEAD + HEAD], joined)
             mean = jnp.mean(u * u, axis=0, keepdims=True)
-            keys[d_tile, at] = (u * lax.rsqrt(mean + 1e-6)).astype(jnp.bfloat16)
+            keys[turn, at] = (u * lax.rsqrt(mean + 1e-6)).astype(jnp.bfloat16)
         tall = jnp.concatenate(
-            [jnp.where(valid[slot][:, :64], upright[slot], 0.0) for slot in range(CAP)], axis=0
+            [jnp.where(valid[slot][:, :64], parts[slot].astype(jnp.float32).T, 0.0)
+             for slot in range(CAP)], axis=0
         ).astype(jnp.bfloat16)
         for at in range(0, HEADS, 2):
             begin = 2 * D + at * HEAD
             v = dot(tall, embed[:, begin : begin + 2 * HEAD]).astype(jnp.bfloat16)
-            values[d_tile, at] = v[:, :HEAD]
-            values[d_tile, at + 1] = v[:, HEAD:]
+            values[turn, at] = v[:, :HEAD]
+            values[turn, at + 1] = v[:, HEAD:]
 
     units = [(at, slot) for at in range(HEADS) for slot in range(CAP)]
-    out_copies = []
     for turn in range(len(units) + 1):
         if turn < len(units):
             at, slot = units[turn]
@@ -280,15 +292,7 @@
                  for part in range(4)], axis=0)
             mixed = dot(soft[(turn - 1) % 3], v)
             final = jnp.where(valid[slot], mixed[:, :HEAD] / mixed[:, HEAD:], 0.0)
-            result[slot, :, at * HEAD : at * HEAD + HEAD] = final.astype(jnp.bfloat16)
-            if slot == CAP - 1 and at % 3 == 2:
-                spot = pl.ds((at - 2) * HEAD, 3 * HEAD)
-                copy = pltpu.make_async_copy(
-                    result.at[:, :, spot], out_hbm.at[0, 0, :, :, spot], out_sem.at[at // 3])
-                copy.start()
-                out_copies.append(copy)
-    for copy in out_copies:
-        copy.wait()
+            result[0, 0, slot, :, at * HEAD : at * HEAD + HEAD] = final.astype(jnp.bfloat16)
 
     @pl.when(has_prev)
     def _():
@@ -306,18 +310,19 @@
 
 
 def fused(features, taps, bias, embed, query_gain, key_gain, bucket, frames):
-    anywhere = pl.BlockSpec(memory_space=pl.ANY)
+    anywhere = pl.BlockSpec(memory_space=pltpu.HBM)
     vector = pl.BlockSpec(memory_space=pltpu.VMEM)
     return pl.pallas_call(
         fused_kernel,
-        out_shape=jax.ShapeDtypeStruct((1, 1, CAP, 128, D), jnp.bfloat16),
-        in_specs=[anywhere, anywhere, anywhere, anywhere, vector, vector, anywhere, anywhere],
-        out_specs=anywhere,
+        out_shape=pltpu.VMEM((1, 1, CAP, 128, D), jnp.bfloat16),
+        in_specs=[anywhere] * 8,
+        out_specs=vector,
         scratch_shapes=[
             pltpu.VMEM((2, 4, 64, 512), jnp.bfloat16),
             pltpu.VMEM((432, 512), jnp.bfloat16),
             pltpu.SMEM((ZC,), jnp.float32),
             pltpu.VMEM((64, 3 * D), jnp.bfloat16),
+            pltpu.VMEM((2, 1, HEAD), jnp.float32),
             pltpu.SMEM((8, 32), jnp.int32),
             pltpu.SMEM((8, 32), jnp.int32),
             pltpu.VMEM((D, 64), jnp.bfloat16),
@@ -328,13 +333,13 @@
             pltpu.VMEM((2, CAP, 64, 128), jnp.bfloat16),
             pltpu.VMEM((2, CAP, 64, 128), jnp.bfloat16),
             pltpu.VMEM((8, CAP, 64, 128), jnp.bfloat16),
+            pltpu.VMEM((CAP, 64, 128), jnp.bfloat16),
             pltpu.VMEM((CAP, HEADS, 128, HEAD), jnp.bfloat16),
             pltpu.VMEM((4, HEADS, HEAD, CAP * 128), jnp.bfloat16),
             pltpu.VMEM((4, HEADS, CAP * 128, HEAD), jnp.bfloat16),
             pltpu.VMEM((CAP, 128, HEAD), jnp.bfloat16),
             pltpu.VMEM((3, 128, 512), jnp.bfloat16),
-            pltpu.VMEM((CAP, 128, D), jnp.bfloat16),
-            pltpu.SemaphoreType.DMA((6,)),
+            pltpu.SemaphoreType.DMA((8,)),
             pltpu.SemaphoreType.DMA((2,)),
             pltpu.SemaphoreType.DMA((2,)),
             pltpu.SemaphoreType.DMA((N_X,)),
@@ -343,11 +348,12 @@
             pltpu.SemaphoreType.DMA((1,)),
             pltpu.SemaphoreType.DMA((8,)),
             pltpu.SemaphoreType.DMA((8,)),
-            pltpu.SemaphoreType.DMA((4,)),
         ],
-        compiler_params=pltpu.CompilerParams(collective_id=0, has_side_effects=True),
+        compiler_params=pltpu.CompilerParams(
+            collective_id=0, has_side_effects=True, vmem_limit_bytes=40 * 2**20),
         name="fused",
-    )(features, taps, bias, embed, query_gain, key_gain, bucket, frames)
+    )(*(pltpu.with_memory_space_constraint(array, pltpu.HBM) for array in (
+        features, taps, bias, embed, query_gain, key_gain, bucket, frames)))
 
 
 def shards(features, conv_weight, conv_bias, embed_qkv, query_gain, key_gain, bucket, frames):

time: 37.6 us -> 36.1 us (0.960)
  local copies, waits for them, and re-layouts: 2.06 us -> 0.88 us
    unnamed x1, local copies, waits for them, and re-layouts: 2.06 us -> 0.88 us
where the time goes in v3:
time: 36.1 us; the launch traced here: 35.9 us
  Pallas kernels  35 us (97%)
  local copies, waits for them, and re-layouts  0.88 us (2%)
    pallas_call x1, Pallas kernels, fused(): pl.pallas_call(fused_kernel, out_shape=pltpu.VMEM((1, 1, CAP, 128, D), jn...  35 us
    unnamed x1, local copies, waits for them, and re-layouts  0.88 us

profile of v3, /device:TPU:3, one launch (start us, length us, event | category | flops | bytes accessed | tf_op | source)
XLA Modules:
  0.0 35.9 jit_solution(12998743866712534330)
XLA Ops:
  0.0 35.0 %fused.1 = bf16[1,1,2,128,1536]{4,3,2,1,0:T(8,128)(2,1)S(1)} custom-call(bf16[2,4,64,512]{3,2,1,0:T(8,128)(2,1)} %bitcast.6, bf16[432,512]{1,0:T(8,128)(2,1)} %bitcast.7, f32[16]{0:T(128)} %bias_hbm.1, bf16[64,4608]{1,0:T(8,128)(2,1)} %embed_hbm.1, f32[1,128]{1,0:T(1,128)} %bitcast.8, f32[1,128]{1,0:T(1,128)} %bitcast.9, s32[8,32]{1,0:T(8,128)} %bucket_hbm.1, ...), custom_call_target="tpu_custom_call" | custom-call | tf_op jit(solution)/shard_map/fused/pallas_call | solution.py:315
  35.0 0.9 %copy.10 = bf16[1,1,2,128,1536]{4,3,2,1,0:T(8,128)(2,1)} copy(bf16[1,1,2,128,1536]{4,3,2,1,0:T(8,128)(2,1)S(1)} %fused.1) | data formatting | bytes 1572864

commit v4 on v3

--- a/solution.py
+++ b/solution.py
@@ -25,7 +25,7 @@
                  frames_hbm, result,
                  feat, taps_ref, bias, embed, gains, bucket, frames, key_rows, halo_out, halo_in,
                  xbuf, pick_out, pick_in, ysum, ybuf, part_now, queries, keys, values, ones, soft,
-                 load_sem, halo_ssem, halo_rsem, x_ssem, x_rsem, c_ssem, c_rsem, y_ssem, y_rsem):
+                 load_sem, halo_ssem, halo_rsem, x_ssem, x_rsem, c_ssem, c_rsem, y_ssem, y_rsem, relay):
     tile = lax.axis_index("tile")
     seq = lax.axis_index("seq")
     group = lax.axis_index("group")
@@ -54,12 +54,28 @@
     ]
     for load in loads:
         load.start()
+    next_x = [at_x(1), at_x(N_X - 1)]
+    next_y = [
+        {"tile": (tile + 1) % n_tile,
+         "group": x_at * 4 + ((hi_at + (tile + 1) // 4) % 2) * 2 + core_at},
+        {"tile": (tile + n_tile - 1) % n_tile,
+         "group": x_at * 4 + ((hi_at + (4 - tile) // 4) % 2) * 2 + core_at},
+    ]
     barrier = pltpu.get_barrier_semaphore()
-    for step in x_steps:
-        pl.semaphore_signal(barrier, inc=1, device_id=at_x(step), device_id_type=MESH)
-    for step in y_steps:
-        pl.semaphore_signal(barrier, inc=1, device_id=at_y(*step), device_id_type=MESH)
-    pl.semaphore_signal(barrier, inc=1, device_id=partner, device_id_type=MESH)
+    for near in next_x + next_y + [partner]:
+        pl.semaphore_signal(barrier, inc=1, device_id=near, device_id_type=MESH)
+
+    def tell(ring, k):
+        for near in (next_x, next_y)[ring]:
+            pl.semaphore_signal(
+                relay.at[ring, k], inc=1, device_id=near, device_id_type=MESH)
+
+    def hear_all(ring):
+        for k in range(3):
+            pl.semaphore_wait(relay.at[ring, k], 2)
+            if k < 2:
+                tell(ring, k + 1)
+
     xbuf[N_X] = jnp.zeros((64, 128), jnp.bfloat16)
     for load in loads[:2]:
         load.wait()
@@ -97,7 +113,7 @@
     halo_in[0] = jnp.where(low_half, part[0][up][0], swap(part[1][up][0]))
     halo_in[1] = jnp.where(low_half, swap(part[0][down][1]), part[1][down][1])
 
-    pl.semaphore_wait(barrier, 15)
+    pl.semaphore_wait(barrier, 5)
 
     to_prev = pltpu.make_async_remote_copy(
         src_ref=halo_out.at[0], dst_ref=halo_in.at[3], send_sem=halo_ssem.at[0],
@@ -117,6 +133,9 @@
     @pl.when(has_next)
     def _():
         to_next.start()
+
+    tell(0, 0)
+    tell(1, 0)
 
     for load in loads[2:5]:
         load.wait()
@@ -141,6 +160,8 @@
     channel = lax.broadcasted_iota(jnp.int32, (ZC, 128), 0)
     for k in range(ZC):
         bias_column = jnp.where(channel == k, bias[k], bias_column)
+
+    hear_all(0)
 
     @pl.when(has_prev)
     def _():
@@ -196,6 +217,7 @@
             mine = (count > slot) & (source % 4 == hi_at * 2 + core_at)
             picks.append(jnp.where(mine, (x_at + N_X - source // 4) % N_X, N_X))
 
+    hear_all(1)
     for load in loads[5:]:
         load.wait()
     for at in range(HEADS):
@@ -348,6 +370,7 @@
             pltpu.SemaphoreType.DMA((1,)),
             pltpu.SemaphoreType.DMA((8,)),
             pltpu.SemaphoreType.DMA((8,)),
+            pltpu.SemaphoreType.REGULAR((2, 3)),
         ],
         compiler_params=pltpu.CompilerParams(
             collective_id=0, has_side_effects=True, vmem_limit_bytes=40 * 2**20),

time: 36.1 us -> 37.9 us (1.050)
  the two profiles are of different devices: /device:TPU:3 before, /device:TPU:1 now
where the time goes in v4:
time: 37.9 us; the launch traced here: 37.8 us
  Pallas kernels  36.9 us (97%)
  local copies, waits for them, and re-layouts  0.88 us (2%)
    pallas_call x1, Pallas kernels, fused(): pl.pallas_call(fused_kernel, out_shape=pltpu.VMEM((1, 1, CAP, 128, D), jn...  36.9 us
    unnamed x1, local copies, waits for them, and re-layouts  0.88 us

profile of v4, /device:TPU:1, one launch (start us, length us, event | category | flops | bytes accessed | tf_op | source)
XLA Modules:
  0.0 37.8 jit_solution(4667411173344136046)
XLA Ops:
  0.0 36.9 %fused.1 = bf16[1,1,2,128,1536]{4,3,2,1,0:T(8,128)(2,1)S(1)} custom-call(bf16[2,4,64,512]{3,2,1,0:T(8,128)(2,1)} %bitcast.6, bf16[432,512]{1,0:T(8,128)(2,1)} %bitcast.7, f32[16]{0:T(128)} %bias_hbm.1, bf16[64,4608]{1,0:T(8,128)(2,1)} %embed_hbm.1, f32[1,128]{1,0:T(1,128)} %bitcast.8, f32[1,128]{1,0:T(1,128)} %bitcast.9, s32[8,32]{1,0:T(8,128)} %bucket_hbm.1, ...), custom_call_target="tpu_custom_call" | custom-call | tf_op jit(solution)/shard_map/fused/pallas_call | solution.py:337
  36.9 0.9 %copy.10 = bf16[1,1,2,128,1536]{4,3,2,1,0:T(8,128)(2,1)} copy(bf16[1,1,2,128,1536]{4,3,2,1,0:T(8,128)(2,1)S(1)} %fused.1) | data formatting | bytes 1572864

commit v5 on v3

--- a/solution.py
+++ b/solution.py
@@ -25,7 +25,7 @@
                  frames_hbm, result,
                  feat, taps_ref, bias, embed, gains, bucket, frames, key_rows, halo_out, halo_in,
                  xbuf, pick_out, pick_in, ysum, ybuf, part_now, queries, keys, values, ones, soft,
-                 load_sem, halo_ssem, halo_rsem, x_ssem, x_rsem, c_ssem, c_rsem, y_ssem, y_rsem):
+                 load_sem, halo_ssem, halo_rsem, x_ssem, x_rsem, c_ssem, c_rsem, y_ssem, y_rsem, relay):
     tile = lax.axis_index("tile")
     seq = lax.axis_index("seq")
     group = lax.axis_index("group")
@@ -54,12 +54,20 @@
     ]
     for load in loads:
         load.start()
+    next_y = [
+        {"tile": (tile + 1) % n_tile,
+         "group": x_at * 4 + ((hi_at + (tile + 1) // 4) % 2) * 2 + core_at},
+        {"tile": (tile + n_tile - 1) % n_tile,
+         "group": x_at * 4 + ((hi_at + (4 - tile) // 4) % 2) * 2 + core_at},
+    ]
     barrier = pltpu.get_barrier_semaphore()
-    for step in x_steps:
-        pl.semaphore_signal(barrier, inc=1, device_id=at_x(step), device_id_type=MESH)
-    for step in y_steps:
-        pl.semaphore_signal(barrier, inc=1, device_id=at_y(*step), device_id_type=MESH)
-    pl.semaphore_signal(barrier, inc=1, device_id=partner, device_id_type=MESH)
+    for near in [at_x(step) for step in x_steps] + next_y + [partner]:
+        pl.semaphore_signal(barrier, inc=1, device_id=near, device_id_type=MESH)
+
+    def tell(k):
+        for near in next_y:
+            pl.semaphore_signal(relay.at[k], inc=1, device_id=near, device_id_type=MESH)
+
     xbuf[N_X] = jnp.zeros((64, 128), jnp.bfloat16)
     for load in loads[:2]:
         load.wait()
@@ -97,7 +105,7 @@
     halo_in[0] = jnp.where(low_half, part[0][up][0], swap(part[1][up][0]))
     halo_in[1] = jnp.where(low_half, swap(part[0][down][1]), part[1][down][1])
 
-    pl.semaphore_wait(barrier, 15)
+    pl.semaphore_wait(barrier, 10)
 
     to_prev = pltpu.make_async_remote_copy(
         src_ref=halo_out.at[0], dst_ref=halo_in.at[3], send_sem=halo_ssem.at[0],
@@ -117,6 +125,8 @@
     @pl.when(has_next)
     def _():
         to_next.start()
+
+    tell(0)
 
     for load in loads[2:5]:
         load.wait()
@@ -196,6 +206,10 @@
             mine = (count > slot) & (source % 4 == hi_at * 2 + core_at)
             picks.append(jnp.where(mine, (x_at + N_X - source // 4) % N_X, N_X))
 
+    for k in range(3):
+        pl.semaphore_wait(relay.at[k], 2)
+        if k < 2:
+            tell(k + 1)
     for load in loads[5:]:
         load.wait()
     for at in range(HEADS):
@@ -348,6 +362,7 @@
             pltpu.SemaphoreType.DMA((1,)),
             pltpu.SemaphoreType.DMA((8,)),
             pltpu.SemaphoreType.DMA((8,)),
+            pltpu.SemaphoreType.REGULAR((3,)),
         ],
         compiler_params=pltpu.CompilerParams(
             collective_id=0, has_side_effects=True, vmem_limit_bytes=40 * 2**20),

time: 36.1 us -> 35 us (0.970)
  the two profiles are of different devices: /device:TPU:3 before, /device:TPU:1 now
where the time goes in v5:
time: 35 us; the launch traced here: 34.9 us
  Pallas kernels  34 us (97%)
  local copies, waits for them, and re-layouts  0.88 us (3%)
    pallas_call x1, Pallas kernels, fused(): pl.pallas_call(fused_kernel, out_shape=pltpu.VMEM((1, 1, CAP, 128, D), jn...  34 us
    unnamed x1, local copies, waits for them, and re-layouts  0.88 us

profile of v5, /device:TPU:1, one launch (start us, length us, event | category | flops | bytes accessed | tf_op | source)
XLA Modules:
  0.0 34.9 jit_solution(15800727892466055732)
XLA Ops:
  0.0 34.0 %fused.1 = bf16[1,1,2,128,1536]{4,3,2,1,0:T(8,128)(2,1)S(1)} custom-call(bf16[2,4,64,512]{3,2,1,0:T(8,128)(2,1)} %bitcast.6, bf16[432,512]{1,0:T(8,128)(2,1)} %bitcast.7, f32[16]{0:T(128)} %bias_hbm.1, bf16[64,4608]{1,0:T(8,128)(2,1)} %embed_hbm.1, f32[1,128]{1,0:T(1,128)} %bitcast.8, f32[1,128]{1,0:T(1,128)} %bitcast.9, s32[8,32]{1,0:T(8,128)} %bucket_hbm.1, ...), custom_call_target="tpu_custom_call" | custom-call | tf_op jit(solution)/shard_map/fused/pallas_call | solution.py:329
  34.0 0.9 %copy.10 = bf16[1,1,2,128,1536]{4,3,2,1,0:T(8,128)(2,1)} copy(bf16[1,1,2,128,1536]{4,3,2,1,0:T(8,128)(2,1)S(1)} %fused.1) | data formatting | bytes 1572864
